TPU v7x, 512 devices: a whole 4x8x8 slice. The times are simulated.
512 devices in a mesh: agent: 16 (over x, z_lo, core), tp: 32 (over z_hi, y).
Axes of the slice: x: 4, y: 8, z: 8 (z_hi: 4, z_lo: 2; z = z_hi * 2 + z_lo), core: 2. Of those that a mesh axis runs over, the one named last changes fastest.
Arguments:
- tokens: bfloat16 [16, 512, 2048], P('agent', 'tp'), may hold values from -6 to 6
- targets: bfloat16 [16, 512, 2048], P('agent', 'tp'), may hold values from -6 to 6
- params: bfloat16 [16, 2048, 8192], P('agent', None, 'tp'), may hold values from -6 to 6
- tracker: bfloat16 [16, 2048, 8192], P('agent', None, 'tp'), may hold values from -6 to 6
- up_weight: bfloat16 [2048, 8192], P('agent', 'tp'), may hold values from -0.125 to 0.125
- down_weight: bfloat16 [8192, 2048], P('tp', 'agent'), may hold values from -0.0625 to 0.0625
- edge_weight: float32 [16], replicated, may hold values from 0.1 to 0.4
- step_size: float32 [1], replicated, may hold values from 0.1 to 0.5
Outputs:
- new_params: bfloat16 [16, 2048, 8192], P('agent', None, 'tp')
- new_tracker: bfloat16 [16, 2048, 8192], P('agent', None, 'tp')
All inputs are finite; a program needn't handle non-finite values.
Results may differ from a plain program's by a relative error of at most 0.033.
Values may be sent and summed in bfloat16 or wider, within the bound.
A program may use at most 64 MiB of HBM per device.

v0:
```python
import jax
import jax.numpy as jnp
from jax import lax
from jax.sharding import Mesh
from jax.sharding import PartitionSpec as P

TP = ("tp_0", "tp_1")


def passed_along(value, axis, steps):
    count = lax.axis_size(axis)
    pairs = [(source, (source + steps) % count) for source in range(count)]
    return lax.ppermute(value, axis, pairs)


def gather_turned(arrays, axis, dims):
    turned = [jnp.moveaxis(a, dim, 0) for a, dim in zip(arrays, dims)]
    widths = [t[0].size for t in turned]
    both = jnp.concatenate([t.reshape(-1, w) for t, w in zip(turned, widths)], axis=1)
    out = lax.all_gather(both, axis, axis=0, tiled=True)
    pieces = jnp.split(out, [sum(widths[:k]) for k in range(1, len(widths))], axis=1)
    return tuple(
        (
            jnp.moveaxis(b.reshape(-1, *t.shape[1:]), 0, dim)
            for b, t, dim in zip(pieces, turned, dims)
        )
    )


def side_by_side(arrays, axis, dim, along):
    widths = [a.shape[along] for a in arrays]
    both = jnp.concatenate(arrays, axis=along)
    out = lax.all_gather(both, axis, axis=dim, tiled=True)
    return tuple(jnp.split(out, [sum(widths[:k]) for k in range(1, len(widths))], axis=along))


def sum_in_order(pieces, axes, turns):
    lengths = [lax.axis_size(a) for a in axes]
    pieces = pieces.reshape(*lengths, *pieces.shape[1:])
    pieces = pieces.transpose(*turns, *range(len(axes), pieces.ndim))
    pieces = pieces.reshape(-1, *pieces.shape[len(axes) :])
    for k in turns:
        pieces = lax.psum_scatter(pieces, axes[k], scatter_dimension=0, tiled=True)
    return pieces[0]


def cut_along(array, dim, devices):
    before, after = (array.shape[:dim], array.shape[dim + 1 :])
    return jnp.moveaxis(array.reshape(*before, devices, -1, *after), dim, 0)


def sum_by_axis(array, axes, turns, dim):
    devices = lax.axis_size(axes)
    return sum_in_order(cut_along(array, dim, devices), axes, turns)


def joined_along(pieces, dim):
    lengths = list(pieces.shape[1:])
    lengths[dim] *= pieces.shape[0]
    return jnp.moveaxis(pieces, 0, dim).reshape(lengths)


def gather_in_order(array, axes, turns):
    pieces = array[None]
    for k in turns:
        pieces = lax.all_gather(pieces, axes[k], axis=0, tiled=True)
    block = [lax.axis_size(axes[k]) for k in reversed(turns)]
    pieces = pieces.reshape(*block, *array.shape)
    turned = sorted(range(len(turns)), key=lambda place: turns[len(turns) - 1 - place])
    return pieces.transpose(*turned, *range(len(turns), pieces.ndim)).reshape(-1, *array.shape)


def gather_axes(array, axes, turns, dim):
    return joined_along(gather_in_order(array, axes, turns), dim)


def on_device(tokens, targets, params, tracker, up_weight, down_weight, edge_weight, step_size):
    target_rows = targets[0]
    param = params[0]
    track = tracker[0]
    left_x, left_y = passed_along((param, track), "agent", 1)
    right_x, right_y = passed_along((param, track), "agent", -1)
    up_full, down_full = gather_turned((up_weight, down_weight), "agent", (0, 1))
    whole, whole_targets = side_by_side((tokens[0], target_rows), TP, 0, 1)
    scale = 1.0 / whole.shape[1] ** 0.5
    up = jnp.dot(whole, up_full, preferred_element_type=jnp.float32)

    def dgate_of(weights):
        gate = jnp.dot(whole, weights, preferred_element_type=jnp.float32) * scale
        sig = jax.nn.sigmoid(gate)
        hidden = (sig * gate * up).astype(jnp.bfloat16)
        partial_value = jnp.dot(hidden, down_full, preferred_element_type=jnp.float32)
        summed = sum_by_axis(partial_value.astype(jnp.bfloat16), TP, (1, 0), 0).astype(jnp.float32)
        local_err = (2.0 * (summed - target_rows.astype(jnp.float32))).astype(jnp.bfloat16)
        err = gather_axes(local_err, TP, (0, 1), 0)
        back = lax.dot_general(
            err, down_full, (((1,), (1,)), ((), ())), preferred_element_type=jnp.float32
        )
        return (back * up * sig * (1.0 + gate * (1.0 - sig))).astype(jnp.bfloat16)

    def weight_grad(dgate):
        return lax.dot_general(
            whole, dgate, (((0,), (0,)), ((), ())), preferred_element_type=jnp.float32
        )

    old_grad = weight_grad(dgate_of(param))
    count = lax.axis_size("agent")
    index = lax.axis_index("agent")
    e_right = lax.dynamic_slice_in_dim(edge_weight, index, 1)[0]
    e_left = lax.dynamic_slice_in_dim(edge_weight, (index + count - 1) % count, 1)[0]
    own = 1.0 - e_right - e_left
    track32 = track.astype(jnp.float32)
    mixed_x = (
        own * param.astype(jnp.float32)
        + e_right * right_x.astype(jnp.float32)
        + e_left * left_x.astype(jnp.float32)
    )
    mixed_y = (
        own * track32 + e_right * right_y.astype(jnp.float32) + e_left * left_y.astype(jnp.float32)
    )
    fresh = (mixed_x - step_size[0] * track32).astype(jnp.bfloat16)
    new_grad = weight_grad(dgate_of(fresh))
    fresh_track = (mixed_y + (new_grad - old_grad) * scale).astype(jnp.bfloat16)
    return (fresh[None], fresh_track[None])


def solution(mesh):
    finer = Mesh(mesh.devices.reshape(mesh.shape["agent"], 4, 8), ("agent", "tp_0", "tp_1"))
    in_specs = (
        P("agent", TP, None),
        P("agent", TP, None),
        P("agent", None, TP),
        P("agent", None, TP),
        P("agent", TP),
        P(TP, "agent"),
        P(),
        P(),
    )
    out_specs = (P("agent", None, TP), P("agent", None, TP))
    return jax.shard_map(
        on_device, mesh=finer, in_specs=in_specs, out_specs=out_specs, check_vma=False
    )
```

profile of v0, /device:TPU:2, one launch (start us, length us, event | category | flops | bytes accessed | tf_op | source)
XLA Modules:
  0.0 443.6 jit_solution(4100841673525199849)
XLA Ops:
  7.2 0.0 all-gather.5.cloned.1.call-start
  7.2 1.5 pad_maximum_fusion
  8.7 0.0 all-gather.5.cloned.1.call-update
  8.8 0.0 all-gather.7.cloned.1.call-start
  8.8 1.0 copy.21
  9.8 1.5 pad_maximum_fusion.1
  11.3 0.0 all-gather.7.cloned.1.call-update
  11.3 0.0 reduce-scatter.5.cloned.1.call-start
  11.4 3.7 collective-permute-start
  15.1 1.9 collective-permute-start.1
  17.6 1.3 fusion.49
  20.2 18.2 %collective-permute-done = bf16[2048,256]{1,0:T(8,128)(2,1)S(1)} collective-permute-done((bf16[2048,256]{1,0:T(8,128)(2,1)}, bf16[2048,256]{1,0:T(8,128)(2,1)S(1)}, u32[]{:S(2)}, u32[]{:S(2)}) %collective-permute-start) | collective-permute-done | bytes 1048608 | tf_op jit(solution)/shard_map/ppermute | solution.py:13
  38.4 4.3 collective-permute-done.1
  42.6 3.5 fusion.2
  46.1 0.0 copy-start.2
  46.1 73.3 %all-gather.5.cloned.1.call-done = bf16[512,4096]{1,0:T(8,128)(2,1)} async-done(((bf16[16,4096]{1,0:T(8,128)(2,1)}), bf16[512,4096]{1,0:T(8,128)(2,1)}) %all-gather.5.cloned.1.call-update) | async-done | bytes 4194320 | tf_op jit(solution)/shard_map/all_gather | solution.py:33
  119.5 2.3 convolution_multiply_fusion.3
  121.8 0.0 copy-done.2
  121.8 0.0 copy-start.7
  121.8 37.5 %all-gather.7.cloned.1.call-done = bf16[2048,512]{0,1:T(8,128)(2,1)} async-done(((bf16[128,512]{0,1:T(8,128)(2,1)}), bf16[2048,512]{0,1:T(8,128)(2,1)}) %all-gather.7.cloned.1.call-update) | async-done | bytes 2097168 | tf_op jit(solution)/shard_map/all_gather | solution.py:20
  159.3 2.7 fusion.15
  162.1 0.0 copy-done.7
  162.1 0.0 copy-done.4
  162.1 0.0 copy-start.5
  162.1 0.7 convolution_convert_fusion.1
  162.8 0.0 copy-done.5
  162.9 1.5 copy.22
  164.4 0.0 reduce-scatter.5.cloned.1.call-update
  164.4 0.0 reduce-scatter.9.cloned.1.call-start
  164.5 1.1 copy-done
  165.6 2.4 convolution_multiply_fusion.1
  168.0 0.0 copy-done.6
  168.0 0.0 copy-start.8
  168.0 0.7 convolution_convert_fusion
  168.8 0.0 copy-done.8
  168.8 1.5 copy.24
  170.3 0.0 reduce-scatter.9.cloned.1.call-update
  170.4 0.0 reduce-scatter.7.cloned.1.call-start
  170.4 39.5 %reduce-scatter.5.cloned.1.call-done = bf16[4,16,2048]{2,1,0:T(8,128)(2,1)} async-done(((bf16[32,16,2048]{2,1,0:T(8,128)(2,1)}), bf16[4,16,2048]{2,1,0:T(8,128)(2,1)}) %reduce-scatter.5.cloned.1.call-update) | async-done | bytes 262160 | tf_op jit(solution)/shard_map/reduce_scatter | solution.py:43
  209.9 0.0 reduce-scatter.7.cloned.1.call-update
  209.9 0.0 reduce-scatter.11.cloned.1.call-start
  210.0 46.5 %reduce-scatter.9.cloned.1.call-done = bf16[4,16,2048]{2,1,0:T(8,128)(2,1)} async-done(((bf16[32,16,2048]{2,1,0:T(8,128)(2,1)}), bf16[4,16,2048]{2,1,0:T(8,128)(2,1)}) %reduce-scatter.9.cloned.1.call-update) | async-done | bytes 262160 | tf_op jit(solution)/shard_map/reduce_scatter | solution.py:43
  256.5 0.0 reduce-scatter.11.cloned.1.call-update
  256.5 0.0 all-gather.9.cloned.1.call-start
  256.6 31.1 %reduce-scatter.7.cloned.1.call-done = bf16[1,16,2048]{2,1,0:T(8,128)(2,1)} async-done(((bf16[4,16,2048]{2,1,0:T(8,128)(2,1)}), bf16[1,16,2048]{2,1,0:T(8,128)(2,1)}) %reduce-scatter.7.cloned.1.call-update) | async-done | bytes 65552 | tf_op jit(solution)/shard_map/reduce_scatter | solution.py:43
  287.7 29.8 %reduce-scatter.11.cloned.1.call-done = bf16[1,16,2048]{2,1,0:T(8,128)(2,1)} async-done(((bf16[4,16,2048]{2,1,0:T(8,128)(2,1)}), bf16[1,16,2048]{2,1,0:T(8,128)(2,1)}) %reduce-scatter.11.cloned.1.call-update) | async-done | bytes 65552 | tf_op jit(solution)/shard_map/reduce_scatter | solution.py:43
  317.4 0.0 copy-done.3
  317.4 0.9 fusion.43
  318.4 16.1 %all_gather.20 = bf16[4,16,2048]{2,1,0:T(8,128)(2,1)} all-gather(bf16[1,16,2048]{2,1,0:T(8,128)(2,1)S(1)} %get-tuple-element.3), channel_id=1, replica_groups=mesh['agent'=16,'tp_0'=4,'tp_1'=8] {'tp_0'}, dimensions={0}, use_global_device_ids=true | all-gather | bytes 327680 | tf_op jit(solution)/shard_map/all_gather | solution.py:66
  334.5 0.0 all-gather.9.cloned.1.call-update
  334.5 0.0 all-gather.11.cloned.1.call-start
  334.5 15.8 %all_gather.22 = bf16[4,16,2048]{2,1,0:T(8,128)(2,1)} all-gather(bf16[1,16,2048]{2,1,0:T(8,128)(2,1)S(1)} %get-tuple-element.2), channel_id=1, replica_groups=mesh['agent'=16,'tp_0'=4,'tp_1'=8] {'tp_0'}, dimensions={0}, use_global_device_ids=true | all-gather | bytes 327680 | tf_op jit(solution)/shard_map/all_gather | solution.py:66
  350.4 0.0 all-gather.11.cloned.1.call-update
  350.4 0.0 copy-done.1
  350.4 1.9 collective-permute-start.2
  352.3 2.4 collective-permute-start.3
  354.7 21.3 %all-gather.9.cloned.1.call-done = bf16[32,16,2048]{2,1,0:T(8,128)(2,1)} async-done(((bf16[4,16,2048]{2,1,0:T(8,128)(2,1)}), bf16[32,16,2048]{2,1,0:T(8,128)(2,1)}) %all-gather.9.cloned.1.call-update) | async-done | bytes 2097168 | tf_op jit(solution)/shard_map/all_gather | solution.py:66
  376.0 3.2 copy.23
  379.2 41.0 %all-gather.11.cloned.1.call-done = bf16[32,16,2048]{2,1,0:T(8,128)(2,1)} async-done(((bf16[4,16,2048]{2,1,0:T(8,128)(2,1)}), bf16[32,16,2048]{2,1,0:T(8,128)(2,1)}) %all-gather.11.cloned.1.call-update) | async-done | bytes 2097168 | tf_op jit(solution)/shard_map/all_gather | solution.py:66
  420.2 1.7 copy.25
  422.0 6.6 %fusion.13 = f32[2048,256]{1,0:T(8,128)} fusion(bf16[512,4096]{1,0:T(8,128)(2,1)} %all-gather.5.cloned.1.call-done, f32[512,256]{1,0:T(8,128)} %copy-done.7, f32[512,256]{1,0:T(8,128)} %copy-done.5, bf16[512,2048]{1,0:T(8,128)(2,1)} %bitcast.41, bf16[2048,512]{0,1:T(8,128)(2,1)} %all-gather.7.cloned.1.call-done), kind=kOutput, calls=%fused_computation.22 | convolution fusion | flops 1075052544 | bytes 8388608 | tf_op jit(solution)/shard_map/dot_general | solution.py:102
  428.6 0.0 collective-permute-done.2
  428.6 0.0 collective-permute-done.3
  428.6 8.2 %fusion.20 = bf16[1,2048,256]{2,1,0:T(8,128)(2,1)} fusion(f32[2048,256]{1,0:T(8,128)} %fusion.13, bf16[512,4096]{1,0:T(8,128)(2,1)} %all-gather.5.cloned.1.call-done, bf16[2048,256]{1,0:T(8,128)(2,1)} %collective-permute-done.3, bf16[2048,256]{1,0:T(8,128)(2,1)} %collective-permute-done.2, f32[]{:T(128)} %bitcast.1, f32[]{:T(128)} %bitcast, f32[]{:T(128)S(6)} %sub.31, ...), kind=kOutput, calls=%fused_computation.27 | convolution fusion | flops 1081344000 | bytes 12583940 | tf_op jit(solution)/shard_map/dot_general | solution.py:102
  (5 shorter events, 0.0 us)
Async XLA Ops:
  7.2 112.3 %all-gather.5.cloned.1.call-start = ((), (), s32[]{:S(2)}) async-start(), calls=%async_computation.4 | async-start | bytes 4325376 | tf_op jit(solution)/shard_map/all_gather | solution.py:33
  8.8 150.5 %all-gather.7.cloned.1.call-start = ((), (), s32[]{:S(2)}) async-start(), calls=%async_computation.5 | async-start | bytes 2228224 | tf_op jit(solution)/shard_map/all_gather | solution.py:20
  11.3 198.6 %reduce-scatter.5.cloned.1.call-start = ((), (), s32[]{:S(2)}) async-start(), calls=%async_computation.6 | async-start | bytes 2359296 | tf_op jit(solution)/shard_map/reduce_scatter | solution.py:43
  11.4 27.0 %collective-permute-start = (bf16[2048,256]{1,0:T(8,128)(2,1)}, bf16[2048,256]{1,0:T(8,128)(2,1)S(1)}, u32[]{:S(2)}, u32[]{:S(2)}) collective-permute-start(bf16[2048,256]{1,0:T(8,128)(2,1)} %bitcast.44), channel_id=1, source_target_pairs={{0,480},{32,0},{64,32},{96,64},{128,96},{160,128},{192,160},{224,1... | collective-permute-start | bytes 3145736 | tf_op jit(solution)/shard_map/ppermute | solution.py:13
  15.1 27.6 %collective-permute-start.1 = (bf16[2048,256]{1,0:T(8,128)(2,1)}, bf16[2048,256]{1,0:T(8,128)(2,1)S(1)}, u32[]{:S(2)}, u32[]{:S(2)}) collective-permute-start(bf16[2048,256]{1,0:T(8,128)(2,1)} %bitcast.45), channel_id=1, source_target_pairs={{0,32},{32,64},{64,96},{96,128},{128,160},{160,192},{192,224},{224... | collective-permute-start | bytes 3145736 | tf_op jit(solution)/shard_map/ppermute | solution.py:13
  46.1 75.7 %copy-start.2 = (bf16[2048,256]{1,0:T(8,128)(2,1)}, bf16[2048,256]{1,0:T(8,128)(2,1)S(1)}, u32[]{:S(2)}) copy-start(bf16[2048,256]{1,0:T(8,128)(2,1)S(1)} %fusion.2) | copy-start | bytes 3145732
  121.8 40.3 %copy-start.7 = (f32[512,256]{1,0:T(8,128)}, f32[512,256]{1,0:T(8,128)S(1)}, u32[]{:S(2)}) copy-start(f32[512,256]{1,0:T(8,128)S(1)} %convolution_multiply_fusion.3) | copy-start | bytes 1572868
  159.3 2.8 copy-start.4
  162.1 0.8 copy-start.5
  164.4 1.2 copy-start
  164.4 92.1 %reduce-scatter.9.cloned.1.call-start = ((), (), s32[]{:S(2)}) async-start(), calls=%async_computation.9 | async-start | bytes 2359296 | tf_op jit(solution)/shard_map/reduce_scatter | solution.py:43
  165.6 2.4 copy-start.6
  168.0 0.8 copy-start.8
  170.3 147.1 %copy-start.3 = (bf16[1,16,2048]{2,1,0:T(8,128)(2,1)S(1)}, bf16[1,16,2048]{2,1,0:T(8,128)(2,1)}, u32[]{:S(2)}) copy-start(bf16[1,16,2048]{2,1,0:T(8,128)(2,1)} %param.9) | copy-start | bytes 196612
  170.3 180.1 %copy-start.1 = (bf16[1,2048,256]{2,1,0:T(8,128)(2,1)S(1)}, bf16[1,2048,256]{2,1,0:T(8,128)(2,1)}, u32[]{:S(2)}) copy-start(bf16[1,2048,256]{2,1,0:T(8,128)(2,1)} %param.11) | copy-start | bytes 3145732
  170.4 117.3 %reduce-scatter.7.cloned.1.call-start = ((), (), s32[]{:S(2)}) async-start(), calls=%async_computation.7 | async-start | bytes 327680 | tf_op jit(solution)/shard_map/reduce_scatter | solution.py:43
  209.9 107.5 %reduce-scatter.11.cloned.1.call-start = ((), (), s32[]{:S(2)}) async-start(), calls=%async_computation.10 | async-start | bytes 327680 | tf_op jit(solution)/shard_map/reduce_scatter | solution.py:43
  256.5 119.5 %all-gather.9.cloned.1.call-start = ((), (), s32[]{:S(2)}) async-start(), calls=%async_computation.8 | async-start | bytes 2359296 | tf_op jit(solution)/shard_map/all_gather | solution.py:66
  334.5 85.8 %all-gather.11.cloned.1.call-start = ((), (), s32[]{:S(2)}) async-start(), calls=%async_computation.11 | async-start | bytes 2359296 | tf_op jit(solution)/shard_map/all_gather | solution.py:66
  350.4 78.2 %collective-permute-start.2 = (bf16[2048,256]{1,0:T(8,128)(2,1)S(1)}, bf16[2048,256]{1,0:T(8,128)(2,1)}, u32[]{:S(2)}, u32[]{:S(2)}) collective-permute-start(bf16[2048,256]{1,0:T(8,128)(2,1)S(1)} %bitcast.46), channel_id=1, source_target_pairs={{0,480},{32,0},{64,32},{96,64},{128,96},{160,128},{192,160},{224,1... | collective-permute-start | bytes 3145736 | tf_op jit(solution)/shard_map/ppermute | solution.py:13
  352.3 76.2 %collective-permute-start.3 = (bf16[2048,256]{1,0:T(8,128)(2,1)S(1)}, bf16[2048,256]{1,0:T(8,128)(2,1)}, u32[]{:S(2)}, u32[]{:S(2)}) collective-permute-start(bf16[2048,256]{1,0:T(8,128)(2,1)S(1)} %bitcast.47), channel_id=1, source_target_pairs={{0,32},{32,64},{64,96},{96,128},{128,160},{160,192},{192,224},{224... | collective-permute-start | bytes 3145736 | tf_op jit(solution)/shard_map/ppermute | solution.py:13
Sparse Core Ops, SparseCore 0:
  11.7 107.7 all-gather.4
  121.5 37.7 all-gather.6
  164.5 45.3 reduce-scatter.4
  212.6 43.8 reduce-scatter.8
  259.1 28.4 reduce-scatter.6
  290.3 27.0 reduce-scatter.10
  334.6 41.3 all-gather.8
  378.1 42.0 all-gather.10
where the time goes:
time: 444 us
  waiting for transfers between devices  343 us (77%)
  blocking collectives  31.9 us (7%)
  matrix products  23.7 us (5%)
  between operations  16.1 us (4%)
  local copies, waits for them, and re-layouts  11.5 us (3%)
  starting transfers between devices  10.3 us (2%)
  other arithmetic  7.43 us (2%)
    reduce_scatter x4, waiting for transfers between devices, sum_in_order(): pieces = lax.psum_scatter(pieces, axes[k], scatter_dimension=0, tiled=True)  147 us
    all_gather x1, waiting for transfers between devices, side_by_side(): out = lax.all_gather(both, axis, axis=dim, tiled=True)  73.3 us
    all_gather x2, waiting for transfers between devices, gather_in_order(): pieces = lax.all_gather(pieces, axes[k], axis=0, tiled=True)  62.3 us
    all_gather x1, waiting for transfers between devices, gather_turned(): out = lax.all_gather(both, axis, axis=0, tiled=True)  37.5 us
    all_gather x2, blocking collectives, gather_in_order(): pieces = lax.all_gather(pieces, axes[k], axis=0, tiled=True)  31.9 us
    ppermute x4, waiting for transfers between devices, passed_along(): return lax.ppermute(value, axis, pairs)  22.5 us
    dot_general x2, matrix products, weight_grad(): lax.dot_general(whole, dgate, (((0,), (0,)), ((), ())), preferred_element...  14.8 us
    ppermute x4, starting transfers between devices, passed_along(): return lax.ppermute(value, axis, pairs)  9.95 us
  transfers between devices with their start and end apart: 12, of which 10 were waited for; matrix products, arithmetic and copies ran while one was open for 6% of the time, Pallas kernels for 0%

commit v1 on v0

--- a/solution.py
+++ b/solution.py
@@ -17,7 +17,9 @@
     turned = [jnp.moveaxis(a, dim, 0) for a, dim in zip(arrays, dims)]
     widths = [t[0].size for t in turned]
     both = jnp.concatenate([t.reshape(-1, w) for t, w in zip(turned, widths)], axis=1)
-    out = lax.all_gather(both, axis, axis=0, tiled=True)
+    out = jnp.concatenate(
+        lax.all_to_all(jnp.stack([both] * lax.axis_size(axis)), axis, 0, 0), axis=0
+    )
     pieces = jnp.split(out, [sum(widths[:k]) for k in range(1, len(widths))], axis=1)
     return tuple(
         (

time: 444 us -> 408 us (0.919)
  waiting for transfers between devices: 343 us -> 295 us
  starting transfers between devices: 10.3 us -> 19.1 us
    all_gather x1 -> x0, waiting for transfers between devices: 37.5 us -> none  [gather_turned(): out = lax.all_gather(both, axis, axis=0, tiled=True)]
    all_gather x1, waiting for transfers between devices: 73.3 us -> 40.6 us  [side_by_side(): out = lax.all_gather(both, axis, axis=dim, tiled=True)]
    ppermute x4, waiting for transfers between devices: 22.5 us -> 47.1 us  [passed_along(): return lax.ppermute(value, axis, pairs)]
    all_to_all x0 -> x1, starting transfers between devices: none -> 9.54 us  [gather_turned(): lax.all_to_all(jnp.stack([both] * lax.axis_size(axis)), axis, 0, 0)]
  transfers between devices with their start and end apart: 12 -> 12, of which waited for: 10 -> 9; matrix products, arithmetic and copies ran while one was open for 6% -> 7% of each run, Pallas kernels for 0% -> 0%
where the time goes in v1:
time: 408 us; the launch traced here: 407 us
  waiting for transfers between devices  295 us (72%)
  blocking collectives  31 us (8%)
  matrix products  24.4 us (6%)
  starting transfers between devices  19.1 us (5%)
  between operations  16.3 us (4%)
  local copies, waits for them, and re-layouts  12.9 us (3%)
  other arithmetic  8.23 us (2%)
    reduce_scatter x4, waiting for transfers between devices, sum_in_order(): pieces = lax.psum_scatter(pieces, axes[k], scatter_dimension=0, tiled=True)  144 us
    all_gather x2, waiting for transfers between devices, gather_in_order(): pieces = lax.all_gather(pieces, axes[k], axis=0, tiled=True)  63 us
    ppermute x4, waiting for transfers between devices, passed_along(): return lax.ppermute(value, axis, pairs)  47.1 us
    all_gather x1, waiting for transfers between devices, side_by_side(): out = lax.all_gather(both, axis, axis=dim, tiled=True)  40.6 us
    all_gather x2, blocking collectives, gather_in_order(): pieces = lax.all_gather(pieces, axes[k], axis=0, tiled=True)  31 us
    dot_general x2, matrix products, weight_grad(): lax.dot_general(whole, dgate, (((0,), (0,)), ((), ())), preferred_element...  14.8 us
    all_to_all x1, starting transfers between devices, gather_turned(): lax.all_to_all(jnp.stack([both] * lax.axis_size(axis)), axis, 0, 0)  9.54 us
    ppermute x4, starting transfers between devices, passed_along(): return lax.ppermute(value, axis, pairs)  9.34 us
  transfers between devices with their start and end apart: 12, of which 9 were waited for; matrix products, arithmetic and copies ran while one was open for 7% of the time, Pallas kernels for 0%

profile of v1, /device:TPU:2, one launch (start us, length us, event | category | flops | bytes accessed | tf_op | source)
XLA Modules:
  0.0 406.9 jit_solution(11137534819100185359)
XLA Ops:
  7.2 0.0 all-gather.4.cloned.1.call-start
  7.2 1.5 pad_maximum_fusion
  8.7 0.0 all-gather.4.cloned.1.call-update
  8.8 1.0 copy.24
  9.7 0.9 pad_maximum_fusion.1
  10.6 0.1 copy.25
  10.7 1.6 stack.2
  12.3 0.0 copy-start
  12.3 9.5 %all-to-all-start = ((bf16[16,128,512]{2,1,0:T(8,128)(2,1)}), bf16[16,128,512]{2,1,0:T(8,128)(2,1)S(1)}, u32[]{:S(2)}, u32[]{:S(2)}) async-start(bf16[16,128,512]{2,1,0:T(8,128)(2,1)} %stack.2), calls=%async_computation | async-start | bytes 4194304 | tf_op jit(solution)/shard_map/all_to_all | solution.py:21
  21.8 0.0 reduce-scatter.5.cloned.1.call-start
  21.8 0.0 copy-done
  21.9 3.1 collective-permute-start
  24.9 1.9 collective-permute-start.1
  27.5 0.0 copy-done.3
  27.6 0.7 fusion.49
  29.6 43.7 %collective-permute-done = bf16[2048,256]{1,0:T(8,128)(2,1)} collective-permute-done((bf16[2048,256]{1,0:T(8,128)(2,1)S(1)}, bf16[2048,256]{1,0:T(8,128)(2,1)}, u32[]{:S(2)}, u32[]{:S(2)}) %collective-permute-start) | collective-permute-done | bytes 1048608 | tf_op jit(solution)/shard_map/ppermute | solution.py:13
  73.2 3.4 collective-permute-done.1
  76.7 4.9 %fusion.2 = bf16[2048,256]{1,0:T(8,128)(2,1)} fusion(bf16[2048,256]{1,0:T(8,128)(2,1)} %collective-permute-done.1, bf16[2048,256]{1,0:T(8,128)(2,1)} %collective-permute-done, f32[]{:T(128)} %bitcast.36, f32[]{:T(128)} %bitcast.1, f32[]{:T(128)} %bitcast, f32[]{:T(128)S(6)} %sub.31, bf16[1,2048,256]{2,1,0:T(8,128)(2,1)} %param.11, ...), kind=kLoop, calls=%fused_computation.7 | loop fusion | flops 6291456 | bytes 5242896 | tf_op jit(solution)/shard_map/convert_element_type | solution.py:123
  81.6 40.6 %all-gather.4.cloned.1.call-done = bf16[512,4096]{1,0:T(8,128)(2,1)} async-done(((bf16[16,4096]{1,0:T(8,128)(2,1)}), bf16[512,4096]{1,0:T(8,128)(2,1)}) %all-gather.4.cloned.1.call-update) | async-done | bytes 4194320 | tf_op jit(solution)/shard_map/all_gather | solution.py:35
  122.2 3.4 convolution_multiply_fusion.3
  125.6 0.0 all-to-all-done
  125.6 2.4 fusion.15
  128.0 0.0 copy-done.6
  128.0 0.0 copy-start.4
  128.0 0.8 convolution_convert_fusion.1
  128.7 0.1 copy-done.4
  128.8 1.5 copy.26
  130.3 0.0 reduce-scatter.5.cloned.1.call-update
  130.3 0.0 reduce-scatter.9.cloned.1.call-start
  130.4 0.0 copy-start.5
  130.4 2.4 convolution_multiply_fusion.1
  132.8 0.0 copy-done.5
  132.8 0.0 copy-start.7
  132.8 0.8 convolution_convert_fusion
  133.5 0.0 copy-done.7
  133.6 1.5 copy.28
  135.1 0.0 reduce-scatter.9.cloned.1.call-update
  135.1 0.0 reduce-scatter.7.cloned.1.call-start
  135.2 36.3 %reduce-scatter.5.cloned.1.call-done = bf16[4,16,2048]{2,1,0:T(8,128)(2,1)} async-done(((bf16[32,16,2048]{2,1,0:T(8,128)(2,1)}), bf16[4,16,2048]{2,1,0:T(8,128)(2,1)}) %reduce-scatter.5.cloned.1.call-update) | async-done | bytes 262160 | tf_op jit(solution)/shard_map/reduce_scatter | solution.py:45
  171.4 0.0 reduce-scatter.7.cloned.1.call-update
  171.4 0.0 reduce-scatter.11.cloned.1.call-start
  171.5 47.1 %reduce-scatter.9.cloned.1.call-done = bf16[4,16,2048]{2,1,0:T(8,128)(2,1)} async-done(((bf16[32,16,2048]{2,1,0:T(8,128)(2,1)}), bf16[4,16,2048]{2,1,0:T(8,128)(2,1)}) %reduce-scatter.9.cloned.1.call-update) | async-done | bytes 262160 | tf_op jit(solution)/shard_map/reduce_scatter | solution.py:45
  218.6 0.0 reduce-scatter.11.cloned.1.call-update
  218.6 0.0 all-gather.6.cloned.1.call-start
  218.6 30.9 %reduce-scatter.7.cloned.1.call-done = bf16[1,16,2048]{2,1,0:T(8,128)(2,1)} async-done(((bf16[4,16,2048]{2,1,0:T(8,128)(2,1)}), bf16[1,16,2048]{2,1,0:T(8,128)(2,1)}) %reduce-scatter.7.cloned.1.call-update) | async-done | bytes 65552 | tf_op jit(solution)/shard_map/reduce_scatter | solution.py:45
  249.6 29.9 %reduce-scatter.11.cloned.1.call-done = bf16[1,16,2048]{2,1,0:T(8,128)(2,1)} async-done(((bf16[4,16,2048]{2,1,0:T(8,128)(2,1)}), bf16[1,16,2048]{2,1,0:T(8,128)(2,1)}) %reduce-scatter.11.cloned.1.call-update) | async-done | bytes 65552 | tf_op jit(solution)/shard_map/reduce_scatter | solution.py:45
  279.4 0.0 copy-done.2
  279.4 0.9 fusion.43
  280.4 15.8 %all_gather.16 = bf16[4,16,2048]{2,1,0:T(8,128)(2,1)} all-gather(bf16[1,16,2048]{2,1,0:T(8,128)(2,1)S(1)} %get-tuple-element.3), channel_id=1, replica_groups=mesh['agent'=16,'tp_0'=4,'tp_1'=8] {'tp_0'}, dimensions={0}, use_global_device_ids=true | all-gather | bytes 327680 | tf_op jit(solution)/shard_map/all_gather | solution.py:68
  296.1 0.0 all-gather.6.cloned.1.call-update
  296.2 0.0 all-gather.8.cloned.1.call-start
  296.2 15.2 %all_gather.18 = bf16[4,16,2048]{2,1,0:T(8,128)(2,1)} all-gather(bf16[1,16,2048]{2,1,0:T(8,128)(2,1)S(1)} %get-tuple-element.2), channel_id=1, replica_groups=mesh['agent'=16,'tp_0'=4,'tp_1'=8] {'tp_0'}, dimensions={0}, use_global_device_ids=true | all-gather | bytes 327680 | tf_op jit(solution)/shard_map/all_gather | solution.py:68
  311.4 0.0 all-gather.8.cloned.1.call-update
  311.5 0.0 copy-done.1
  311.5 1.9 collective-permute-start.2
  313.4 2.4 collective-permute-start.3
  315.8 22.0 %all-gather.6.cloned.1.call-done = bf16[32,16,2048]{2,1,0:T(8,128)(2,1)} async-done(((bf16[4,16,2048]{2,1,0:T(8,128)(2,1)}), bf16[32,16,2048]{2,1,0:T(8,128)(2,1)}) %all-gather.6.cloned.1.call-update) | async-done | bytes 2097168 | tf_op jit(solution)/shard_map/all_gather | solution.py:68
  337.8 3.2 copy.27
  341.1 41.0 %all-gather.8.cloned.1.call-done = bf16[32,16,2048]{2,1,0:T(8,128)(2,1)} async-done(((bf16[4,16,2048]{2,1,0:T(8,128)(2,1)}), bf16[32,16,2048]{2,1,0:T(8,128)(2,1)}) %all-gather.8.cloned.1.call-update) | async-done | bytes 2097168 | tf_op jit(solution)/shard_map/all_gather | solution.py:68
  382.1 3.2 copy.29
  385.3 6.2 %fusion.13 = f32[2048,256]{1,0:T(8,128)} fusion(bf16[512,4096]{1,0:T(8,128)(2,1)} %all-gather.4.cloned.1.call-done, f32[512,256]{1,0:T(8,128)} %convolution_multiply_fusion.3, f32[512,256]{1,0:T(8,128)} %copy-done.4, bf16[512,2048]{1,0:T(8,128)(2,1)} %bitcast.47, bf16[2048,512]{1,0:T(8,128)(2,1)S(1)} %bitcast.42), kind=kOutput, calls=%fused_computation.22 | convolution fusion | flops 1075052544 | bytes 8388608 | tf_op jit(solution)/shard_map/dot_general | solution.py:104
  391.5 0.0 collective-permute-done.2
  391.5 0.0 collective-permute-done.3
  391.5 8.6 %fusion.20 = bf16[1,2048,256]{2,1,0:T(8,128)(2,1)} fusion(f32[2048,256]{1,0:T(8,128)} %fusion.13, bf16[512,4096]{1,0:T(8,128)(2,1)} %all-gather.4.cloned.1.call-done, bf16[2048,256]{1,0:T(8,128)(2,1)} %collective-permute-done.3, bf16[2048,256]{1,0:T(8,128)(2,1)} %collective-permute-done.2, f32[]{:T(128)} %bitcast.1, f32[]{:T(128)} %bitcast, f32[]{:T(128)S(6)} %sub.31, ...), kind=kOutput, calls=%fused_computation.27 | convolution fusion | flops 1081344000 | bytes 12583940 | tf_op jit(solution)/shard_map/dot_general | solution.py:104
  (4 shorter events, 0.0 us)
Async XLA Ops:
  7.2 115.1 %all-gather.4.cloned.1.call-start = ((), (), s32[]{:S(2)}) async-start(), calls=%async_computation.5 | async-start | bytes 4325376 | tf_op jit(solution)/shard_map/all_gather | solution.py:35
  12.3 9.6 %copy-start = (bf16[1,2048,256]{2,1,0:T(8,128)(2,1)S(1)}, bf16[1,2048,256]{2,1,0:T(8,128)(2,1)}, u32[]{:S(2)}) copy-start(bf16[1,2048,256]{2,1,0:T(8,128)(2,1)} %param.10) | copy-start | bytes 3145732
  12.3 15.3 %copy-start.3 = (f32[16]{0:T(128)S(1)}, f32[16]{0:T(128)}, u32[]{:S(2)}) copy-start(f32[16]{0:T(128)} %param.14) | copy-start | bytes 196
  12.3 113.3 %all-to-all-start = ((bf16[16,128,512]{2,1,0:T(8,128)(2,1)}), bf16[16,128,512]{2,1,0:T(8,128)(2,1)S(1)}, u32[]{:S(2)}, u32[]{:S(2)}) async-start(bf16[16,128,512]{2,1,0:T(8,128)(2,1)} %stack.2), calls=%async_computation | async-start | bytes 4194304 | tf_op jit(solution)/shard_map/all_to_all | solution.py:21
  21.8 149.6 %reduce-scatter.5.cloned.1.call-start = ((), (), s32[]{:S(2)}) async-start(), calls=%async_computation.6 | async-start | bytes 2359296 | tf_op jit(solution)/shard_map/reduce_scatter | solution.py:45
  21.9 51.4 %collective-permute-start = (bf16[2048,256]{1,0:T(8,128)(2,1)S(1)}, bf16[2048,256]{1,0:T(8,128)(2,1)}, u32[]{:S(2)}, u32[]{:S(2)}) collective-permute-start(bf16[2048,256]{1,0:T(8,128)(2,1)S(1)} %bitcast.50), channel_id=1, source_target_pairs={{0,480},{32,0},{64,32},{96,64},{128,96},{160,128},{192,160},{224,1... | collective-permute-start | bytes 3145736 | tf_op jit(solution)/shard_map/ppermute | solution.py:13
  24.9 51.7 %collective-permute-start.1 = (bf16[2048,256]{1,0:T(8,128)(2,1)S(1)}, bf16[2048,256]{1,0:T(8,128)(2,1)}, u32[]{:S(2)}, u32[]{:S(2)}) collective-permute-start(bf16[2048,256]{1,0:T(8,128)(2,1)S(1)} %bitcast.51), channel_id=1, source_target_pairs={{0,32},{32,64},{64,96},{96,128},{128,160},{160,192},{192,224},{224... | collective-permute-start | bytes 3145736 | tf_op jit(solution)/shard_map/ppermute | solution.py:13
  125.6 2.4 copy-start.6
  128.0 0.9 copy-start.4
  130.3 88.2 %reduce-scatter.9.cloned.1.call-start = ((), (), s32[]{:S(2)}) async-start(), calls=%async_computation.9 | async-start | bytes 2359296 | tf_op jit(solution)/shard_map/reduce_scatter | solution.py:45
  130.4 2.4 copy-start.5
  132.8 0.8 copy-start.7
  135.1 144.4 %copy-start.2 = (bf16[1,16,2048]{2,1,0:T(8,128)(2,1)S(1)}, bf16[1,16,2048]{2,1,0:T(8,128)(2,1)}, u32[]{:S(2)}) copy-start(bf16[1,16,2048]{2,1,0:T(8,128)(2,1)} %param.9) | copy-start | bytes 196612
  135.1 176.4 %copy-start.1 = (bf16[1,2048,256]{2,1,0:T(8,128)(2,1)S(1)}, bf16[1,2048,256]{2,1,0:T(8,128)(2,1)}, u32[]{:S(2)}) copy-start(bf16[1,2048,256]{2,1,0:T(8,128)(2,1)} %param.11) | copy-start | bytes 3145732
  135.1 114.5 %reduce-scatter.7.cloned.1.call-start = ((), (), s32[]{:S(2)}) async-start(), calls=%async_computation.7 | async-start | bytes 327680 | tf_op jit(solution)/shard_map/reduce_scatter | solution.py:45
  171.4 108.0 %reduce-scatter.11.cloned.1.call-start = ((), (), s32[]{:S(2)}) async-start(), calls=%async_computation.10 | async-start | bytes 327680 | tf_op jit(solution)/shard_map/reduce_scatter | solution.py:45
  218.6 119.3 %all-gather.6.cloned.1.call-start = ((), (), s32[]{:S(2)}) async-start(), calls=%async_computation.8 | async-start | bytes 2359296 | tf_op jit(solution)/shard_map/all_gather | solution.py:68
  296.2 85.9 %all-gather.8.cloned.1.call-start = ((), (), s32[]{:S(2)}) async-start(), calls=%async_computation.11 | async-start | bytes 2359296 | tf_op jit(solution)/shard_map/all_gather | solution.py:68
  311.5 80.0 %collective-permute-start.2 = (bf16[2048,256]{1,0:T(8,128)(2,1)S(1)}, bf16[2048,256]{1,0:T(8,128)(2,1)}, u32[]{:S(2)}, u32[]{:S(2)}) collective-permute-start(bf16[2048,256]{1,0:T(8,128)(2,1)S(1)} %bitcast.52), channel_id=1, source_target_pairs={{0,480},{32,0},{64,32},{96,64},{128,96},{160,128},{192,160},{224,1... | collective-permute-start | bytes 3145736 | tf_op jit(solution)/shard_map/ppermute | solution.py:13
  313.4 78.1 %collective-permute-start.3 = (bf16[2048,256]{1,0:T(8,128)(2,1)S(1)}, bf16[2048,256]{1,0:T(8,128)(2,1)}, u32[]{:S(2)}, u32[]{:S(2)}) collective-permute-start(bf16[2048,256]{1,0:T(8,128)(2,1)S(1)} %bitcast.53), channel_id=1, source_target_pairs={{0,32},{32,64},{64,96},{96,128},{128,160},{160,192},{192,224},{224... | collective-permute-start | bytes 3145736 | tf_op jit(solution)/shard_map/ppermute | solution.py:13
Sparse Core Ops, SparseCore 0:
  11.7 110.4 all-gather.3
  130.5 40.9 reduce-scatter.4
  174.3 44.2 reduce-scatter.8
  221.2 28.3 reduce-scatter.6
  252.2 27.1 reduce-scatter.10
  296.3 41.5 all-gather.5
  339.9 42.0 all-gather.7
